TPU v7x, 256 devices: a whole 4x4x8 slice. The times are simulated.
256 devices in a mesh: expert: 64 (over x, z, core), tensor: 4 (over y).
Axes of the slice: x: 4, y: 4, z: 8, core: 2. Of those that a mesh axis runs over, the one named last changes fastest.
Arguments:
- tokens: bfloat16 [8192, 3584], P('expert', 'tensor'), may hold values from -6 to 6
- expert_ids: int32 [8192, 4], P('expert'), may hold values from 0 to 63, all different within a row; in each aligned block of 128 rows (0 to 127, 128 to 255, ...) at most 12 rows name the same one
- gate_values: bfloat16 [8192, 4], P('expert'), may hold values from 0.049804688 to 0.3984375
- w_gate: bfloat16 [64, 3584, 1024], P('expert', None, 'tensor'), may hold values from -0.09375 to 0.09375
- w_up: bfloat16 [64, 3584, 1024], P('expert', None, 'tensor'), may hold values from -0.09375 to 0.09375
- w_down: bfloat16 [64, 1024, 3584], P('expert', 'tensor'), may hold values from -0.1875 to 0.1875
- shared_gate: bfloat16 [3584, 1024], P(None, 'tensor'), may hold values from -0.09375 to 0.09375
- shared_up: bfloat16 [3584, 1024], P(None, 'tensor'), may hold values from -0.09375 to 0.09375
- shared_down: bfloat16 [1024, 3584], P('tensor'), may hold values from -0.1875 to 0.1875
Outputs:
- moe_output: bfloat16 [8192, 3584], P('expert', 'tensor')
Inputs may be any that keep to these rules, and one draw needn't show every extreme that they name: `expert_ids`: each token names 4 different experts. Among the 128 tokens of one index of the expert axis (aligned blocks of 128 rows) no expert is named by more than 12 tokens, a bound that some block reaches.
All inputs are finite; a program needn't handle non-finite values.
Results may differ from a plain program's by a relative error of at most 0.013.
Values may be sent and summed in bfloat16 or wider, within the bound.
No kernel may reach another device: no remote copies, remote signals or barrier semaphores. Data moves between devices by JAX's collectives and lax.ppermute only.
A program may use at most 64 MiB of HBM per device.

v0:
```python
import jax
import jax.numpy as jnp
from jax import lax
from jax.sharding import Mesh
from jax.sharding import PartitionSpec as P

EXPERT = ("expert_0", "expert_1", "expert_2")


def in_order(tiles, dim):
    shape = list(tiles.shape[1:])
    shape[dim] *= tiles.shape[0]
    return jnp.moveaxis(tiles, 0, dim).reshape(shape)


def from_everyone(x, axis):
    copies = jnp.broadcast_to(x, (lax.axis_size(axis), *x.shape))
    return lax.all_to_all(copies, axis, split_axis=0, concat_axis=0, tiled=True)


def collect(x, axis, dim):
    return in_order(from_everyone(x, axis), dim)


def in_blocks(x, dim, devices):
    before, after = (x.shape[:dim], x.shape[dim + 1 :])
    return jnp.moveaxis(x.reshape(*before, devices, -1, *after), dim, 0)


def sent_and_summed(x, axis, dim):
    tiles = in_blocks(x, dim, lax.axis_size(axis))
    arrived = lax.all_to_all(tiles, axis, split_axis=0, concat_axis=0, tiled=True)
    return arrived.astype(jnp.float32).sum(axis=0)


def turned_blocks(tiles, axes, sequence):
    shape = [lax.axis_size(a) for a in axes]
    tiles = tiles.reshape(*shape, *tiles.shape[1:])
    for k in sequence:
        tiles = lax.all_to_all(tiles, axes[k], split_axis=k, concat_axis=k, tiled=True)
    return tiles.reshape(-1, *tiles.shape[len(axes) :])


def core_and_chips(x, groups, sequence, split_dim, concat_dim):
    devices = lax.axis_size(groups[0]) * lax.axis_size(groups[1])
    tiles = in_blocks(x, split_dim, devices)
    return in_order(turned_blocks(tiles, groups, sequence), concat_dim)


def per_device(
    tokens, expert_ids, gate_values, w_gate, w_up, w_down, shared_gate, shared_up, shared_down
):
    tok_dev, narrow = tokens.shape
    top_count = expert_ids.shape[1]
    per_lane, features, quarter = w_gate.shape
    lane_count = lax.axis_size(EXPERT)
    experts_all = lane_count * per_lane
    capacity = min(tok_dev, 3 * tok_dev * top_count // (2 * experts_all))
    total_rows = experts_all * capacity
    numbers = jnp.arange(experts_all, dtype=jnp.int32)
    onehot = (expert_ids[:, :, None] == numbers).astype(jnp.int32)
    per_token = jnp.sum(onehot, axis=1)
    earlier = jnp.cumsum(per_token, axis=0) - per_token
    slot_index = jnp.sum(onehot * earlier[:, None, :], axis=2)
    target = expert_ids * capacity + slot_index
    token_index = jnp.repeat(jnp.arange(tok_dev, dtype=jnp.int32), top_count)
    owners = jnp.full((total_rows,), tok_dev, jnp.int32).at[target.reshape(-1)].set(token_index)
    features_all = collect(tokens, "tensor", 1)
    shared_gate_sums = jnp.dot(features_all, shared_gate, preferred_element_type=jnp.float32)
    shared_up_sums = jnp.dot(features_all, shared_up, preferred_element_type=jnp.float32)
    shared_hidden = (jax.nn.silu(shared_gate_sums) * shared_up_sums).astype(jnp.bfloat16)
    shared_partial = jnp.dot(shared_hidden, shared_down, preferred_element_type=jnp.float32)
    padded = jnp.concatenate([tokens, jnp.zeros((1, narrow), jnp.bfloat16)], axis=0)
    outgoing = padded[owners].reshape(lane_count, per_lane * capacity, narrow)
    arrived = lax.all_to_all(outgoing, EXPERT, split_axis=0, concat_axis=0, tiled=True)
    arrived = arrived.reshape(lane_count, per_lane, capacity, narrow)
    block_rows = lax.all_gather(arrived, "tensor", axis=3, tiled=True)
    gate_more = jnp.einsum("sjcd,jdf->sjcf", block_rows, w_gate, preferred_element_type=jnp.float32)
    up_more = jnp.einsum("sjcd,jdf->sjcf", block_rows, w_up, preferred_element_type=jnp.float32)
    hidden = (jax.nn.silu(gate_more) * up_more).astype(jnp.bfloat16)
    partial_value = jnp.einsum("sjcf,jfd->sjcd", hidden, w_down, preferred_element_type=jnp.float32)
    summed = sent_and_summed(partial_value.astype(jnp.bfloat16), "tensor", 3)
    returned = core_and_chips(
        summed.reshape(lane_count, per_lane * capacity, narrow).astype(jnp.bfloat16),
        (("expert_0", "expert_1"), "expert_2"),
        (1, 0),
        0,
        0,
    ).astype(jnp.float32)
    picked = returned.reshape(total_rows, narrow)[target]
    routed = jnp.sum(gate_values.astype(jnp.float32)[:, :, None] * picked, axis=1)
    shared_total = sent_and_summed(shared_partial.astype(jnp.bfloat16), "tensor", 1)
    return (routed + shared_total).astype(jnp.bfloat16)


def solution(mesh):
    torus = Mesh(
        mesh.devices.reshape(4, 8, 2, mesh.shape["tensor"]),
        ("expert_0", "expert_1", "expert_2", "tensor"),
    )
    placed = (
        P(EXPERT, "tensor"),
        P(EXPERT, None),
        P(EXPERT, None),
        P(EXPERT, None, "tensor"),
        P(EXPERT, None, "tensor"),
        P(EXPERT, "tensor", None),
        P(None, "tensor"),
        P(None, "tensor"),
        P("tensor", None),
    )
    return jax.shard_map(
        per_device, mesh=torus, in_specs=placed, out_specs=P(EXPERT, "tensor"), check_vma=False
    )
```

profile of v0, /device:TPU:32, one launch (start us, length us, event | category | flops | bytes accessed | tf_op | source)
XLA Modules:
  0.0 321.1 jit_solution(12613605834629810689)
XLA Ops:
  6.5 0.8 convert_reduce_fusion.1
  7.7 0.7 select_reduce_fusion
  8.5 0.7 compare_select_fusion.2
  9.5 2.4 scatter_custom_fusion
  12.0 1.0 concatenate.3
  12.9 2.8 gather_fusion
  15.8 1.4 reshape.100
  17.2 56.0 %all_to_all.30 = bf16[64,12,896]{2,1,0:T(8,128)(2,1)S(1)} all-to-all(bf16[64,12,896]{2,1,0:T(8,128)(2,1)} %reshape.100), channel_id=1, replica_groups=mesh['expert_0'=4,'expert_1'=8,'expert_2'=2,'tensor'=4] {'expert_0','exp..., dimensions={0} | all-to-all | bytes 2752512 | tf_op jit(solution)/shard_map/all_to_all | solution.py:75
  73.2 1.4 copy.49
  74.9 1.1 broadcast_in_dim.25
  75.9 4.5 %all-to-all-start.4 = ((bf16[4,128,896]{1,2,0:T(8,128)(2,1)}), bf16[4,128,896]{1,2,0:T(8,128)(2,1)S(1)}, u32[]{:S(2)}, u32[]{:S(2)}) async-start(bf16[4,128,896]{1,2,0:T(8,128)(2,1)} %broadcast_in_dim.25), calls=%async_computation.4 | async-start | bytes 1835008 | tf_op jit(solution)/shard_map/all_to_all | solution.py:18
  80.4 58.3 %all-gather.3.cloned.1.call-done = bf16[64,12,3584]{2,0,1:T(8,128)(2,1)} async-done(((bf16[64,12,896]{2,0,1:T(8,128)(2,1)}), bf16[64,12,3584]{2,0,1:T(8,128)(2,1)}) %all-gather.3.cloned.1.call-update) | async-done | bytes 5505040 | tf_op jit(solution)/shard_map/all_gather | solution.py:77
  138.6 5.6 %fusion.5 = f32[64,1,12,256]{3,0,2,1:T(8,128)} fusion(bf16[64,12,3584]{2,0,1:T(8,128)(2,1)} %all-gather.3.cloned.1.call-done, bf16[1,3584,256]{2,1,0:T(8,128)(2,1)} %param.12), kind=kOutput, calls=%fused_computation.14 | convolution fusion | flops 1409286144 | bytes 8126464 | tf_op jit(solution)/shard_map/sjcd,jdf->sjcf/dot_general | solution.py:78
  144.3 11.5 %convolution_convert_fusion = bf16[64,12,3584]{2,0,1:T(8,128)(2,1)} fusion(bf16[1,256,3584]{2,1,0:T(8,128)(2,1)S(1)} %copy-done, bf16[64,12,3584]{2,0,1:T(8,128)(2,1)} %all-gather.3.cloned.1.call-done, bf16[1,3584,256]{2,1,0:T(8,128)(2,1)} %param.13, f32[64,1,12,256]{3,0,2,1:T(8,128)} %fusion.5), kind=kOutput, calls=%fused_computation.3 | convolution fusion | flops 2822504448 | bytes 15466496 | tf_op jit(solution)/shard_map/sjcf,jfd->sjcd/dot_general | solution.py:81
  155.7 5.8 %copy.65 = bf16[1,12,8,4,8,896]{5,4,2,1,0,3:T(8,128)(2,1)} copy(bf16[1,12,8,4,8,896]{5,4,3,2,1,0:T(8,128)(2,1)} %bitcast.85) | data formatting | bytes 11010048 | tf_op jit(solution)/shard_map/reshape | solution.py:27
  161.6 5.4 %all-to-all-start.1 = ((bf16[4,64,1,12,896]{4,1,3,2,0:T(8,128)(2,1)}), bf16[4,64,1,12,896]{4,1,3,2,0:T(8,128)(2,1)}, u32[]{:S(2)}, u32[]{:S(2)}) async-start(bf16[4,64,1,12,896]{4,1,3,2,0:T(8,128)(2,1)} %bitcast.82), calls=%async_computation.1 | async-start | bytes 11010048 | tf_op jit(solution)/shard_map/all_to_all | solution.py:32
  167.5 3.3 %convolution_convert_fusion.1 = bf16[128,3584]{1,0:T(8,128)(2,1)S(1)} fusion(bf16[256,3584]{1,0:T(8,128)(2,1)} %param.17, bf16[128,3584]{0,1:T(8,128)(2,1)S(1)} %bitcast.84, bf16[3584,256]{1,0:T(8,128)(2,1)} %param.16, f32[128,256]{1,0:T(8,128)S(1)} %fusion.39), kind=kOutput, calls=%fused_computation.5 | convolution fusion | flops 470417408 | bytes 5636096 | tf_op jit(solution)/shard_map/dot_general | solution.py:72
  170.8 1.0 copy.66
  171.8 58.3 %all-to-all-done.1 = bf16[4,64,1,12,896]{4,1,3,2,0:T(8,128)(2,1)} async-done(((bf16[4,64,1,12,896]{4,1,3,2,0:T(8,128)(2,1)}), bf16[4,64,1,12,896]{4,1,3,2,0:T(8,128)(2,1)}, u32[]{:S(2)}, u32[]{:S(2)}) %all-to-all-start.1) | async-done | bytes 5505056 | tf_op jit(solution)/shard_map/all_to_all | solution.py:32
  230.1 3.6 %reduce_sum.50 = bf16[64,12,896]{2,0,1:T(8,128)(2,1)S(1)} reduce(bf16[4,64,1,12,896]{4,1,3,2,0:T(8,128)(2,1)} %all-to-all-done.1, bf16[]{:T(256)} %constant.8.clone.1), dimensions={0,2}, to_apply=%region_4.5 | reduce | flops 2064384 | bytes 6881282 | tf_op jit(solution)/shard_map/reduce_sum | solution.py:33
  234.5 4.8 %all_to_all.31 = bf16[32,2,1,12,896]{4,0,3,2,1:T(8,128)(2,1)S(1)} all-to-all(bf16[32,2,1,12,896]{4,0,3,2,1:T(8,128)(2,1)S(1)} %copy.52), channel_id=1, replica_groups=mesh['expert_0'=4,'expert_1'=8,'expert_2'=2,'tensor'=4] {'expert_2'}, dimensions={1} | all-to-all | bytes 2752512 | tf_op jit(solution)/shard_map/all_to_all | solution.py:40
  239.3 3.5 %all-to-all-start.5 = ((bf16[4,128,896]{2,1,0:T(8,128)(2,1)}), bf16[4,128,896]{2,1,0:T(8,128)(2,1)S(1)}, u32[]{:S(2)}, u32[]{:S(2)}) async-start(bf16[4,128,896]{2,1,0:T(8,128)(2,1)} %bitcast.81), calls=%async_computation.5 | async-start | bytes 1835008 | tf_op jit(solution)/shard_map/all_to_all | solution.py:32
  242.8 2.5 copy.53
  245.3 11.7 %all-to-all-done.5 = bf16[4,128,896]{2,1,0:T(8,128)(2,1)S(1)} async-done(((bf16[4,128,896]{2,1,0:T(8,128)(2,1)}), bf16[4,128,896]{2,1,0:T(8,128)(2,1)S(1)}, u32[]{:S(2)}, u32[]{:S(2)}) %all-to-all-start.5) | async-done | bytes 917536 | tf_op jit(solution)/shard_map/all_to_all | solution.py:32
  257.1 6.9 %all-to-all-start.3 = ((bf16[32,2,1,12,896]{4,1,3,2,0:T(2,128)(2,1)}), bf16[32,2,1,12,896]{4,1,3,2,0:T(2,128)(2,1)S(1)}, u32[]{:S(2)}, u32[]{:S(2)}) async-start(bf16[32,2,1,12,896]{4,1,3,2,0:T(2,128)(2,1)} %copy.53), calls=%async_computation.3 | async-start | bytes 2752512 | tf_op jit(solution)/shard_map/all_to_all | solution.py:40
  264.4 34.2 %all-to-all-done.3 = bf16[32,2,1,12,896]{4,1,3,2,0:T(2,128)(2,1)S(1)} async-done(((bf16[32,2,1,12,896]{4,1,3,2,0:T(2,128)(2,1)}), bf16[32,2,1,12,896]{4,1,3,2,0:T(2,128)(2,1)S(1)}, u32[]{:S(2)}, u32[]{:S(2)}) %all-to-all-start.3) | async-done | bytes 1376288 | tf_op jit(solution)/shard_map/all_to_all | solution.py:40
  299.0 3.4 %copy.55 = f32[32,2,1,12,896]{4,3,1,0,2:T(8,128)} copy(f32[32,2,1,12,896]{4,0,3,2,1:T(8,128)S(1)} %copy_convert_fusion) | data formatting | bytes 5505024 | tf_op jit(solution)/shard_map/convert_element_type | solution.py:89
  302.4 2.9 reshape.110
  305.3 2.7 gather_fusion.1
  307.9 2.9 reshape.120
  310.9 2.7 multiply_reduce_fusion
  313.6 0.7 add_convert_fusion
  (34 shorter events, 2.9 us)
Async XLA Ops:
  6.5 137.7 %copy-start = (bf16[1,256,3584]{2,1,0:T(8,128)(2,1)S(1)}, bf16[1,256,3584]{2,1,0:T(8,128)(2,1)}, u32[]{:S(2)}) copy-start(bf16[1,256,3584]{2,1,0:T(8,128)(2,1)} %param.14) | copy-start | bytes 5505028
  6.5 132.1 %all-gather.3.cloned.1.call-start = ((), (), s32[]{:S(2)}) async-start(), calls=%async_computation.6 | async-start | bytes 6881280 | tf_op jit(solution)/shard_map/all_gather | solution.py:77
  73.2 1.4 copy-start.3
  75.9 85.7 %all-to-all-start.4 = ((bf16[4,128,896]{1,2,0:T(8,128)(2,1)}), bf16[4,128,896]{1,2,0:T(8,128)(2,1)S(1)}, u32[]{:S(2)}, u32[]{:S(2)}) async-start(bf16[4,128,896]{1,2,0:T(8,128)(2,1)} %broadcast_in_dim.25), calls=%async_computation.4 | async-start | bytes 1835008 | tf_op jit(solution)/shard_map/all_to_all | solution.py:18
  161.6 5.5 %copy-start.2 = (bf16[3584,256]{1,0:T(8,128)(2,1)S(1)}, bf16[3584,256]{1,0:T(8,128)(2,1)}, u32[]{:S(2)}) copy-start(bf16[3584,256]{1,0:T(8,128)(2,1)} %param.15) | copy-start | bytes 5505028
  161.6 68.5 %all-to-all-start.1 = ((bf16[4,64,1,12,896]{4,1,3,2,0:T(8,128)(2,1)}), bf16[4,64,1,12,896]{4,1,3,2,0:T(8,128)(2,1)}, u32[]{:S(2)}, u32[]{:S(2)}) async-start(bf16[4,64,1,12,896]{4,1,3,2,0:T(8,128)(2,1)} %bitcast.82), calls=%async_computation.1 | async-start | bytes 11010048 | tf_op jit(solution)/shard_map/all_to_all | solution.py:32
  239.3 17.7 %all-to-all-start.5 = ((bf16[4,128,896]{2,1,0:T(8,128)(2,1)}), bf16[4,128,896]{2,1,0:T(8,128)(2,1)S(1)}, u32[]{:S(2)}, u32[]{:S(2)}) async-start(bf16[4,128,896]{2,1,0:T(8,128)(2,1)} %bitcast.81), calls=%async_computation.5 | async-start | bytes 1835008 | tf_op jit(solution)/shard_map/all_to_all | solution.py:32
  245.3 18.8 %copy-start.4 = (bf16[128,4]{0,1:T(4,128)(2,1)S(1)}, bf16[128,4]{0,1:T(4,128)(2,1)}, u32[]{:S(2)}) copy-start(bf16[128,4]{0,1:T(4,128)(2,1)} %param.11) | copy-start | bytes 3076
  257.1 41.6 %all-to-all-start.3 = ((bf16[32,2,1,12,896]{4,1,3,2,0:T(2,128)(2,1)}), bf16[32,2,1,12,896]{4,1,3,2,0:T(2,128)(2,1)S(1)}, u32[]{:S(2)}, u32[]{:S(2)}) async-start(bf16[32,2,1,12,896]{4,1,3,2,0:T(2,128)(2,1)} %copy.53), calls=%async_computation.3 | async-start | bytes 2752512 | tf_op jit(solution)/shard_map/all_to_all | solution.py:40
  307.9 6.4 %copy-start.1 = (bf16[1,256,3584]{2,1,0:T(8,128)(2,1)S(1)}, bf16[1,256,3584]{2,1,0:T(8,128)(2,1)}, u32[]{:S(2)}) copy-start(bf16[1,256,3584]{2,1,0:T(8,128)(2,1)} %param.14) | copy-start | bytes 5505028
Sparse Core Ops, SparseCore 0:
  74.8 63.8 all-gather.2
where the time goes:
time: 322 us; the launch traced here: 321 us
  waiting for transfers between devices  163 us (51%)
  blocking collectives  60.9 us (19%)
  local copies, waits for them, and re-layouts  33.1 us (10%)
  matrix products  20.8 us (6%)
  starting transfers between devices  20.3 us (6%)
  between operations  13.6 us (4%)
  other arithmetic  9.92 us (3%)
    all_to_all x2, waiting for transfers between devices, sent_and_summed(): lax.all_to_all(tiles, axis, split_axis=0, concat_axis=0, tiled=True)  70.1 us
    all_gather x1, waiting for transfers between devices, per_device(): block_rows = lax.all_gather(arrived, 'tensor', axis=3, tiled=True)  58.3 us
    all_to_all x1, blocking collectives, per_device(): lax.all_to_all(outgoing, EXPERT, split_axis=0, concat_axis=0, tiled=True)  56 us
    all_to_all x1, waiting for transfers between devices, turned_blocks(): lax.all_to_all(tiles, axes[k], split_axis=k, concat_axis=k, tiled=True)  34.2 us
    dot_general x1, matrix products, per_device(): jnp.einsum('sjcf,jfd->sjcd', hidden, w_down, preferred_element_type=jnp.f...  11.5 us
    all_to_all x2, starting transfers between devices, sent_and_summed(): lax.all_to_all(tiles, axis, split_axis=0, concat_axis=0, tiled=True)  8.94 us
    all_to_all x1, starting transfers between devices, turned_blocks(): lax.all_to_all(tiles, axes[k], split_axis=k, concat_axis=k, tiled=True)  6.87 us
    reshape x2, local copies, waits for them, and re-layouts, in_blocks(): return jnp.moveaxis(x.reshape(*before, devices, -1, *after), dim, 0)  6.86 us
  transfers between devices with their start and end apart: 5, of which 4 were waited for; matrix products, arithmetic and copies ran while one was open for 10% of the time, Pallas kernels for 0%

commit v1 on v0

--- a/solution.py
+++ b/solution.py
@@ -74,7 +74,15 @@
     outgoing = padded[owners].reshape(lane_count, per_lane * capacity, narrow)
     arrived = lax.all_to_all(outgoing, EXPERT, split_axis=0, concat_axis=0, tiled=True)
     arrived = arrived.reshape(lane_count, per_lane, capacity, narrow)
-    block_rows = lax.all_gather(arrived, "tensor", axis=3, tiled=True)
+    block_rows = jnp.concatenate(
+        lax.all_to_all(
+            jnp.stack([arrived] * lax.axis_size("tensor")),
+            axis_name="tensor",
+            split_axis=0,
+            concat_axis=0,
+        ),
+        axis=3,
+    )
     gate_more = jnp.einsum("sjcd,jdf->sjcf", block_rows, w_gate, preferred_element_type=jnp.float32)
     up_more = jnp.einsum("sjcd,jdf->sjcf", block_rows, w_up, preferred_element_type=jnp.float32)
     hidden = (jax.nn.silu(gate_more) * up_more).astype(jnp.bfloat16)

time: 322 us -> 339 us (1.053)
  local copies, waits for them, and re-layouts: 33.1 us -> 54 us
  between operations: 13.6 us -> 0.23 us
  starting transfers between devices: 20.3 us -> 25 us
  waiting for transfers between devices: 163 us -> 167 us
    all_to_all x0 -> x1, waiting for transfers between devices: none -> 63.3 us  [per_device(): lax.all_to_all(jnp.stack([arrived] * lax.axis_size('tensor')), axis_name=...]
    all_gather x1 -> x0, waiting for transfers between devices: 58.3 us -> none  [per_device(): block_rows = lax.all_gather(arrived, 'tensor', axis=3, tiled=True)]
    another operation x0 -> x2, local copies, waits for them, and re-layouts: none -> 12.7 us
    reshape x0 -> x1, local copies, waits for them, and re-layouts: none -> 9.27 us  [per_device(): jnp.concatenate(lax.all_to_all(jnp.stack([arrived] * lax.axis_size('tenso...]
    all_to_all x0 -> x1, starting transfers between devices: none -> 5.22 us  [per_device(): lax.all_to_all(jnp.stack([arrived] * lax.axis_size('tensor')), axis_name=...]
  transfers between devices with their start and end apart: 5 -> 5, of which waited for: 4 -> 4; matrix products, arithmetic and copies ran while one was open for 10% -> 15% of each run, Pallas kernels for 0% -> 0%
where the time goes in v1:
time: 339 us; the launch traced here: 338 us
  waiting for transfers between devices  167 us (49%)
  blocking collectives  60.9 us (18%)
  local copies, waits for them, and re-layouts  54 us (16%)
  starting transfers between devices  25 us (7%)
  matrix products  20.8 us (6%)
  other arithmetic  9.92 us (3%)
    all_to_all x2, waiting for transfers between devices, sent_and_summed(): lax.all_to_all(tiles, axis, split_axis=0, concat_axis=0, tiled=True)  69.4 us
    all_to_all x1, waiting for transfers between devices, per_device(): lax.all_to_all(jnp.stack([arrived] * lax.axis_size('tensor')), axis_name=...  63.3 us
    all_to_all x1, blocking collectives, per_device(): lax.all_to_all(outgoing, EXPERT, split_axis=0, concat_axis=0, tiled=True)  56 us
    all_to_all x1, waiting for transfers between devices, turned_blocks(): lax.all_to_all(tiles, axes[k], split_axis=k, concat_axis=k, tiled=True)  34.2 us
    dot_general x1, matrix products, per_device(): jnp.einsum('sjcf,jfd->sjcd', hidden, w_down, preferred_element_type=jnp.f...  11.5 us
    another operation x1, local copies, waits for them, and re-layouts  9.47 us
    reshape x1, local copies, waits for them, and re-layouts, per_device(): jnp.concatenate(lax.all_to_all(jnp.stack([arrived] * lax.axis_size('tenso...  9.27 us
    all_to_all x2, starting transfers between devices, sent_and_summed(): lax.all_to_all(tiles, axis, split_axis=0, concat_axis=0, tiled=True)  8.98 us
  transfers between devices with their start and end apart: 5, of which 4 were waited for; matrix products, arithmetic and copies ran while one was open for 15% of the time, Pallas kernels for 0%

profile of v1, /device:TPU:32, one launch (start us, length us, event | category | flops | bytes accessed | tf_op | source)
XLA Modules:
  0.0 337.8 jit_solution(10408534605004385266)
XLA Ops:
  0.0 0.8 convert_reduce_fusion.1
  3.0 2.4 scatter_custom_fusion
  5.4 1.0 concatenate.3
  6.4 2.8 gather_fusion
  9.2 1.4 reshape.105
  10.7 56.0 %all_to_all.35 = bf16[64,12,896]{2,1,0:T(8,128)(2,1)S(1)} all-to-all(bf16[64,12,896]{2,1,0:T(8,128)(2,1)} %reshape.105), channel_id=1, replica_groups=mesh['expert_0'=4,'expert_1'=8,'expert_2'=2,'tensor'=4] {'expert_0','exp..., dimensions={0} | all-to-all | bytes 2752512 | tf_op jit(solution)/shard_map/all_to_all | solution.py:75
  67.0 3.2 stack.3
  70.2 5.2 %all-to-all-start.1 = ((bf16[4,64,1,12,896]{4,1,3,2,0:T(8,128)(2,1)}), bf16[4,64,1,12,896]{4,1,3,2,0:T(8,128)(2,1)}, u32[]{:S(2)}, u32[]{:S(2)}) async-start(bf16[4,64,1,12,896]{4,1,3,2,0:T(8,128)(2,1)} %stack.3), calls=%async_computation.1 | async-start | bytes 11010048 | tf_op jit(solution)/shard_map/all_to_all | solution.py:78
  75.7 63.3 %all-to-all-done.1 = bf16[4,64,1,12,896]{4,1,3,2,0:T(8,128)(2,1)} async-done(((bf16[4,64,1,12,896]{4,1,3,2,0:T(8,128)(2,1)}), bf16[4,64,1,12,896]{4,1,3,2,0:T(8,128)(2,1)}, u32[]{:S(2)}, u32[]{:S(2)}) %all-to-all-start.1) | async-done | bytes 5505056 | tf_op jit(solution)/shard_map/all_to_all | solution.py:78
  138.9 1.1 broadcast_in_dim.25
  140.0 3.7 %all-to-all-start.5 = ((bf16[4,128,896]{1,2,0:T(8,128)(2,1)}), bf16[4,128,896]{1,2,0:T(8,128)(2,1)S(1)}, u32[]{:S(2)}, u32[]{:S(2)}) async-start(bf16[4,128,896]{1,2,0:T(8,128)(2,1)} %broadcast_in_dim.25), calls=%async_computation.5 | async-start | bytes 1835008 | tf_op jit(solution)/shard_map/all_to_all | solution.py:18
  143.7 9.3 %copy.53 = bf16[64,1,12,4,896]{4,3,0,2,1:T(4,128)(2,1)} copy(bf16[64,1,12,4,896]{4,0,2,1,3:T(8,128)(2,1)} %bitcast.1) | data formatting | bytes 11010048 | tf_op jit(solution)/shard_map/reshape | solution.py:77
  152.9 9.5 %reshape.107 = bf16[64,12,3584]{2,0,1:T(8,128)(2,1)} reshape(bf16[64,1,12,4,896]{4,3,0,2,1:T(4,128)(2,1)} %copy.53) | data formatting | bytes 11010048 | tf_op jit(solution)/shard_map/reshape.2
  162.4 5.6 %fusion.5 = f32[64,1,12,256]{3,0,2,1:T(8,128)} fusion(bf16[64,12,3584]{2,0,1:T(8,128)(2,1)} %reshape.107, bf16[1,3584,256]{2,1,0:T(8,128)(2,1)} %param.12), kind=kOutput, calls=%fused_computation.14 | convolution fusion | flops 1409286144 | bytes 8126464 | tf_op jit(solution)/shard_map/sjcd,jdf->sjcf/dot_general | solution.py:86
  168.0 11.5 %convolution_convert_fusion = bf16[64,12,3584]{2,0,1:T(8,128)(2,1)} fusion(bf16[1,256,3584]{2,1,0:T(8,128)(2,1)S(1)} %copy-done, bf16[64,12,3584]{2,0,1:T(8,128)(2,1)} %reshape.107, bf16[1,3584,256]{2,1,0:T(8,128)(2,1)} %param.13, f32[64,1,12,256]{3,0,2,1:T(8,128)} %fusion.5), kind=kOutput, calls=%fused_computation.3 | convolution fusion | flops 2822504448 | bytes 15466496 | tf_op jit(solution)/shard_map/sjcf,jfd->sjcd/dot_general | solution.py:89
  179.5 5.8 %copy.69 = bf16[1,12,8,4,8,896]{5,4,2,1,0,3:T(8,128)(2,1)} copy(bf16[1,12,8,4,8,896]{5,4,3,2,1,0:T(8,128)(2,1)} %bitcast.88) | data formatting | bytes 11010048 | tf_op jit(solution)/shard_map/reshape | solution.py:27
  185.4 5.5 %all-to-all-start.2 = ((bf16[4,64,1,12,896]{4,1,3,2,0:T(8,128)(2,1)}), bf16[4,64,1,12,896]{4,1,3,2,0:T(8,128)(2,1)}, u32[]{:S(2)}, u32[]{:S(2)}) async-start(bf16[4,64,1,12,896]{4,1,3,2,0:T(8,128)(2,1)} %bitcast.85), calls=%async_computation.2 | async-start | bytes 11010048 | tf_op jit(solution)/shard_map/all_to_all | solution.py:32
  191.3 3.3 convolution_convert_fusion.1
  194.6 1.0 copy.70
  195.6 57.7 %all-to-all-done.2 = bf16[4,64,1,12,896]{4,1,3,2,0:T(8,128)(2,1)} async-done(((bf16[4,64,1,12,896]{4,1,3,2,0:T(8,128)(2,1)}), bf16[4,64,1,12,896]{4,1,3,2,0:T(8,128)(2,1)}, u32[]{:S(2)}, u32[]{:S(2)}) %all-to-all-start.2) | async-done | bytes 5505056 | tf_op jit(solution)/shard_map/all_to_all | solution.py:32
  253.3 3.6 %reduce_sum.50 = bf16[64,12,896]{2,0,1:T(8,128)(2,1)S(1)} reduce(bf16[4,64,1,12,896]{4,1,3,2,0:T(8,128)(2,1)} %all-to-all-done.2, bf16[]{:T(256)} %constant.8.clone.1), dimensions={0,2}, to_apply=%region_4.5 | reduce | flops 2064384 | bytes 6881282 | tf_op jit(solution)/shard_map/reduce_sum | solution.py:33
  257.6 4.8 %all_to_all.36 = bf16[32,2,1,12,896]{4,0,3,2,1:T(8,128)(2,1)S(1)} all-to-all(bf16[32,2,1,12,896]{4,0,3,2,1:T(8,128)(2,1)S(1)} %copy.56), channel_id=1, replica_groups=mesh['expert_0'=4,'expert_1'=8,'expert_2'=2,'tensor'=4] {'expert_2'}, dimensions={1} | all-to-all | bytes 2752512 | tf_op jit(solution)/shard_map/all_to_all | solution.py:40
  262.5 3.5 %all-to-all-start.6 = ((bf16[4,128,896]{2,1,0:T(8,128)(2,1)}), bf16[4,128,896]{2,1,0:T(8,128)(2,1)S(1)}, u32[]{:S(2)}, u32[]{:S(2)}) async-start(bf16[4,128,896]{2,1,0:T(8,128)(2,1)} %bitcast.84), calls=%async_computation.6 | async-start | bytes 1835008 | tf_op jit(solution)/shard_map/all_to_all | solution.py:32
  266.0 2.5 copy.57
  268.5 11.7 %all-to-all-done.6 = bf16[4,128,896]{2,1,0:T(8,128)(2,1)S(1)} async-done(((bf16[4,128,896]{2,1,0:T(8,128)(2,1)}), bf16[4,128,896]{2,1,0:T(8,128)(2,1)S(1)}, u32[]{:S(2)}, u32[]{:S(2)}) %all-to-all-start.6) | async-done | bytes 917536 | tf_op jit(solution)/shard_map/all_to_all | solution.py:32
  280.2 7.2 %all-to-all-start.4 = ((bf16[32,2,1,12,896]{4,1,3,2,0:T(2,128)(2,1)}), bf16[32,2,1,12,896]{4,1,3,2,0:T(2,128)(2,1)S(1)}, u32[]{:S(2)}, u32[]{:S(2)}) async-start(bf16[32,2,1,12,896]{4,1,3,2,0:T(2,128)(2,1)} %copy.57), calls=%async_computation.4 | async-start | bytes 2752512 | tf_op jit(solution)/shard_map/all_to_all | solution.py:40
  287.9 34.2 %all-to-all-done.4 = bf16[32,2,1,12,896]{4,1,3,2,0:T(2,128)(2,1)S(1)} async-done(((bf16[32,2,1,12,896]{4,1,3,2,0:T(2,128)(2,1)}), bf16[32,2,1,12,896]{4,1,3,2,0:T(2,128)(2,1)S(1)}, u32[]{:S(2)}, u32[]{:S(2)}) %all-to-all-start.4) | async-done | bytes 1376288 | tf_op jit(solution)/shard_map/all_to_all | solution.py:40
  322.4 3.4 %copy.59 = f32[32,2,1,12,896]{4,3,1,0,2:T(8,128)} copy(f32[32,2,1,12,896]{4,0,3,2,1:T(8,128)S(1)} %copy_convert_fusion) | data formatting | bytes 5505024 | tf_op jit(solution)/shard_map/convert_element_type | solution.py:97
  325.9 2.9 reshape.115
  328.7 2.7 gather_fusion.1
  331.4 2.9 reshape.125
  334.3 2.7 multiply_reduce_fusion
  (36 shorter events, 5.3 us)
Async XLA Ops:
  0.0 168.0 %copy-start = (bf16[1,256,3584]{2,1,0:T(8,128)(2,1)S(1)}, bf16[1,256,3584]{2,1,0:T(8,128)(2,1)}, u32[]{:S(2)}) copy-start(bf16[1,256,3584]{2,1,0:T(8,128)(2,1)} %param.14) | copy-start | bytes 5505028
  70.2 5.2 %copy-start.3 = (bf16[128,896]{1,0:T(8,128)(2,1)S(1)}, bf16[128,896]{1,0:T(8,128)(2,1)}, u32[]{:S(2)}) copy-start(bf16[128,896]{1,0:T(8,128)(2,1)} %param.9) | copy-start | bytes 688132
  70.2 68.7 %all-to-all-start.1 = ((bf16[4,64,1,12,896]{4,1,3,2,0:T(8,128)(2,1)}), bf16[4,64,1,12,896]{4,1,3,2,0:T(8,128)(2,1)}, u32[]{:S(2)}, u32[]{:S(2)}) async-start(bf16[4,64,1,12,896]{4,1,3,2,0:T(8,128)(2,1)} %stack.3), calls=%async_computation.1 | async-start | bytes 11010048 | tf_op jit(solution)/shard_map/all_to_all | solution.py:78
  140.0 45.4 %all-to-all-start.5 = ((bf16[4,128,896]{1,2,0:T(8,128)(2,1)}), bf16[4,128,896]{1,2,0:T(8,128)(2,1)S(1)}, u32[]{:S(2)}, u32[]{:S(2)}) async-start(bf16[4,128,896]{1,2,0:T(8,128)(2,1)} %broadcast_in_dim.25), calls=%async_computation.5 | async-start | bytes 1835008 | tf_op jit(solution)/shard_map/all_to_all | solution.py:18
  185.4 5.5 %copy-start.2 = (bf16[3584,256]{1,0:T(8,128)(2,1)S(1)}, bf16[3584,256]{1,0:T(8,128)(2,1)}, u32[]{:S(2)}) copy-start(bf16[3584,256]{1,0:T(8,128)(2,1)} %param.15) | copy-start | bytes 5505028
  185.4 67.9 %all-to-all-start.2 = ((bf16[4,64,1,12,896]{4,1,3,2,0:T(8,128)(2,1)}), bf16[4,64,1,12,896]{4,1,3,2,0:T(8,128)(2,1)}, u32[]{:S(2)}, u32[]{:S(2)}) async-start(bf16[4,64,1,12,896]{4,1,3,2,0:T(8,128)(2,1)} %bitcast.85), calls=%async_computation.2 | async-start | bytes 11010048 | tf_op jit(solution)/shard_map/all_to_all | solution.py:32
  262.5 17.7 %all-to-all-start.6 = ((bf16[4,128,896]{2,1,0:T(8,128)(2,1)}), bf16[4,128,896]{2,1,0:T(8,128)(2,1)S(1)}, u32[]{:S(2)}, u32[]{:S(2)}) async-start(bf16[4,128,896]{2,1,0:T(8,128)(2,1)} %bitcast.84), calls=%async_computation.6 | async-start | bytes 1835008 | tf_op jit(solution)/shard_map/all_to_all | solution.py:32
  268.5 19.1 %copy-start.4 = (bf16[128,4]{0,1:T(4,128)(2,1)S(1)}, bf16[128,4]{0,1:T(4,128)(2,1)}, u32[]{:S(2)}) copy-start(bf16[128,4]{0,1:T(4,128)(2,1)} %param.11) | copy-start | bytes 3076
  280.2 41.9 %all-to-all-start.4 = ((bf16[32,2,1,12,896]{4,1,3,2,0:T(2,128)(2,1)}), bf16[32,2,1,12,896]{4,1,3,2,0:T(2,128)(2,1)S(1)}, u32[]{:S(2)}, u32[]{:S(2)}) async-start(bf16[32,2,1,12,896]{4,1,3,2,0:T(2,128)(2,1)} %copy.57), calls=%async_computation.4 | async-start | bytes 2752512 | tf_op jit(solution)/shard_map/all_to_all | solution.py:40
  331.4 6.4 %copy-start.1 = (bf16[1,256,3584]{2,1,0:T(8,128)(2,1)S(1)}, bf16[1,256,3584]{2,1,0:T(8,128)(2,1)}, u32[]{:S(2)}) copy-start(bf16[1,256,3584]{2,1,0:T(8,128)(2,1)} %param.14) | copy-start | bytes 5505028
